TPU v7x, 32 devices: a whole 2x2x4 slice. The times are simulated.
32 devices in a mesh: seq: 8 (over y, x, core), head: 4 (over z).
Axes of the slice: x: 2, y: 2, z: 4, core: 2. Of those that a mesh axis runs over, the one named last changes fastest.
Arguments:
- video_rows: bfloat16 [4096, 5120], P('seq'), may hold values from -6 to 6
- context: bfloat16 [512, 5120], P('seq'), may hold values from -6 to 6
- valid_length: int32 [1], replicated, may hold values from 64 to 512
- timestep: int32 [1], replicated, may hold values from 0 to 999
- query_weight: bfloat16 [5120, 1024], P('seq', 'head'), may hold values from -0.078125 to 0.078125
- key_weight: bfloat16 [5120, 1024], P('seq', 'head'), may hold values from -0.078125 to 0.078125
- value_weight: bfloat16 [5120, 1024], P('seq', 'head'), may hold values from -0.078125 to 0.078125
- out_weight: bfloat16 [1024, 5120], P('head', 'seq'), may hold values from -0.1875 to 0.1875
- query_gain: float32 [1024], P('head'), may hold values from 0.5 to 15
- key_gain: float32 [1024], P('head'), may hold values from 0.5 to 15
- time_weight: bfloat16 [2, 256, 5120], P(None, None, 'head'), may hold values from -0.375 to 0.375
- modulation: float32 [2, 5120], P(None, 'head'), may hold values from -3 to 3
Outputs:
- residual_out: bfloat16 [4096, 5120], P('seq', 'head')
- modulated: bfloat16 [4096, 5120], P('seq', 'head')
Inputs may be any that keep to these rules, and one draw needn't show every extreme that they name: `valid_length`: text positions at or beyond it are padding.
All inputs are finite; a program needn't handle non-finite values.
Results may differ from a plain program's by a relative error of at most 0.0065.
The roundings to bfloat16 on the way count: a program that leaves them out, or rounds other values in their place, can miss the bound.
Values may be sent and summed in bfloat16 or wider, within the bound.
A program may use at most 64 MiB of HBM per device.

v0:
```python
import jax
import jax.numpy as jnp
from jax import lax
from jax.sharding import PartitionSpec as P

HD = 128
FREQ = 256


def layer_norm(rows):
    mean = jnp.mean(rows, axis=-1, keepdims=True)
    spread = jnp.mean((rows - mean) ** 2, axis=-1, keepdims=True)
    return (rows - mean) / jnp.sqrt(spread + 1e-06)


def add_rows(left, piece):
    return jnp.dot(left, piece, preferred_element_type=jnp.float32)


def project_pair(source, key_weight):
    empty = jnp.zeros((source.shape[0], key_weight.shape[1]), jnp.float32)

    def add_both(totals, pieces, start):
        return (add_rows(source, pieces[0]), add_rows(source, pieces[1]))

    return (empty, add_both)


def on_device(
    video_rows,
    context,
    valid_length,
    timestep,
    query_weight,
    key_weight,
    value_weight,
    out_weight,
    query_gain,
    key_gain,
    time_weight,
    modulation,
):
    tok_rows = video_rows.shape[0]
    local_att = query_weight.shape[1]
    width_local = modulation.shape[1]
    heads_local = local_att // HD
    normed = layer_norm(video_rows.astype(jnp.float32)).astype(jnp.bfloat16)
    queries = add_rows(normed, lax.all_gather(query_weight, "seq", axis=0, tiled=True))
    whole_text = lax.all_gather(context, "seq", axis=0, tiled=True)
    empty, add_both = project_pair(whole_text, key_weight)
    key_proj, value_full = add_both(
        (empty, empty),
        (
            lax.all_gather(key_weight, "seq", axis=0, tiled=True),
            lax.all_gather(value_weight, "seq", axis=0, tiled=True),
        ),
        jnp.int32(0),
    )
    query_sq, key_sq = lax.psum(
        (jnp.sum(queries * queries, axis=1), jnp.sum(key_proj * key_proj, axis=1)), "head"
    )
    total_att = local_att * lax.axis_size("head")
    query_normed = (queries / jnp.sqrt(query_sq[:, None] / total_att + 1e-06) * query_gain).astype(
        jnp.bfloat16
    )
    key_normed = (key_proj / jnp.sqrt(key_sq[:, None] / total_att + 1e-06) * key_gain).astype(
        jnp.bfloat16
    )
    value_proj = value_full.astype(jnp.bfloat16)
    text_count = key_normed.shape[0]
    key_valid = jnp.arange(text_count, dtype=jnp.int32) < valid_length[0]
    query_heads = query_normed.reshape(tok_rows, heads_local, HD)
    key_heads = key_normed.reshape(text_count, heads_local, HD)
    value_heads = value_proj.reshape(text_count, heads_local, HD)
    scores = jnp.einsum(
        "thd,shd->hts", query_heads, key_heads, preferred_element_type=jnp.float32
    ) * HD ** (-0.5)
    scores = jnp.where(key_valid[None, None, :], scores, jnp.float32(-1e30))
    shifted = jnp.exp(scores - jnp.max(scores, axis=-1, keepdims=True))
    weights = (shifted / jnp.sum(shifted, axis=-1, keepdims=True)).astype(jnp.bfloat16)
    attended = jnp.einsum(
        "hts,shd->thd", weights, value_heads, preferred_element_type=jnp.float32
    ).astype(jnp.bfloat16)
    attended = attended.reshape(tok_rows, local_att)
    wide_rows = lax.all_gather(out_weight, "seq", axis=1, tiled=True)
    block_rows = lax.all_to_all(wide_rows, "head", split_axis=1, concat_axis=0, tiled=True)
    projected = jnp.dot(
        lax.all_gather(attended, "head", axis=1, tiled=True),
        block_rows,
        preferred_element_type=jnp.float32,
    )
    video_part = lax.dynamic_slice_in_dim(
        video_rows, lax.axis_index("head") * width_local, width_local, 1
    )
    residual_out = (video_part.astype(jnp.float32) + projected).astype(jnp.bfloat16)
    half = FREQ // 2
    freqs = jnp.exp(-jnp.log(10000.0) * jnp.arange(half, dtype=jnp.float32) / half)
    angles = timestep[0].astype(jnp.float32) * freqs
    embedding = jnp.concatenate([jnp.cos(angles), jnp.sin(angles)])
    act = jax.nn.silu(embedding).astype(jnp.bfloat16)[None, :]
    shift = modulation[0] + jnp.dot(act, time_weight[0], preferred_element_type=jnp.float32)[0]
    scale = modulation[1] + jnp.dot(act, time_weight[1], preferred_element_type=jnp.float32)[0]
    resid = residual_out.astype(jnp.float32)
    row_sum, row_squares = lax.psum(
        (jnp.sum(resid, axis=1), jnp.sum(resid * resid, axis=1)), "head"
    )
    full_width = width_local * lax.axis_size("head")
    mean2 = (row_sum / full_width)[:, None]
    var2 = (row_squares / full_width)[:, None] - mean2 * mean2
    modulated = ((resid - mean2) / jnp.sqrt(var2 + 1e-06) * (1.0 + scale) + shift).astype(
        jnp.bfloat16
    )
    return (residual_out, modulated)


def solution(mesh):
    in_specs = (
        P("seq", None),
        P("seq", None),
        P(),
        P(),
        P("seq", "head"),
        P("seq", "head"),
        P("seq", "head"),
        P("head", "seq"),
        P("head"),
        P("head"),
        P(None, None, "head"),
        P(None, "head"),
    )
    out_specs = (P("seq", "head"), P("seq", "head"))
    return jax.shard_map(
        on_device, mesh=mesh, in_specs=in_specs, out_specs=out_specs, check_vma=False
    )
```

profile of v0, /device:TPU:0, one launch (start us, length us, event | category | flops | bytes accessed | tf_op | source)
XLA Modules:
  0.0 240.9 jit_solution(14338393817382619489)
XLA Ops:
  7.2 0.0 all-gather.17.cloned.1.call-start
  7.2 1.9 copy.23
  9.1 0.0 all-gather.11.cloned.1.call-start
  9.2 0.7 all-gather.11.cloned.1.call-update
  9.9 0.7 all-gather.13.cloned.1.call-update
  10.6 0.5 all-gather.7.cloned.1.call-update
  11.2 0.0 all-gather.9.cloned.1.call-start
  11.2 0.5 all-gather.9.cloned.1.call-update
  12.4 3.4 %convert_reduce_fusion = f32[512]{0:T(512)S(1)} fusion(bf16[512,5120]{1,0:T(8,128)(2,1)} %param.12), kind=kLoop, calls=%fused_computation.2 | loop fusion | flops 5242368 | bytes 5244928 | tf_op jit(solution)/shard_map/reduce_sum | solution.py:11
  15.8 0.6 copy-done
  16.5 1.5 fusion.3
  18.0 25.2 %all-gather.17.cloned.1.call-done = bf16[256,5120]{0,1:T(8,128)(2,1)} async-done(((bf16[256,640]{0,1:T(8,128)(2,1)}), bf16[256,5120]{0,1:T(8,128)(2,1)}) %all-gather.17.cloned.1.call-update) | async-done | bytes 2621456 | tf_op jit(solution)/shard_map/all_gather | solution.py:85
  43.2 4.6 %all-to-all-start = ((bf16[256,4,1280]{0,2,1:T(8,128)(2,1)}), bf16[256,4,1280]{0,2,1:T(8,128)(2,1)S(1)}, u32[]{:S(2)}, u32[]{:S(2)}) async-start(bf16[256,4,1280]{0,2,1:T(8,128)(2,1)} %bitcast.33), calls=%async_computation | async-start | bytes 5242880 | tf_op jit(solution)/shard_map/all_to_all | solution.py:86
  47.8 27.3 %all-gather.11.cloned.1.call-done = bf16[5120,256]{1,0:T(8,128)(2,1)} async-done(((bf16[640,256]{1,0:T(8,128)(2,1)}), bf16[5120,256]{1,0:T(8,128)(2,1)}) %all-gather.11.cloned.1.call-update) | async-done | bytes 2621456 | tf_op jit(solution)/shard_map/all_gather | solution.py:48
  75.1 5.3 %multiply_reduce_fusion.1 = (f32[512]{0:T(512)S(1)}, f32[512,256]{0,1:T(8,128)S(1)}) fusion(bf16[5120,256]{1,0:T(8,128)(2,1)} %all-gather.11.cloned.1.call-done, bf16[512,5120]{1,0:T(8,128)(2,1)} %param.12, f32[512]{0:T(512)S(1)} %add_sqrt_fusion.3, f32[512]{0:T(512)S(1)} %broadcast_multiply_fusion.1), kind=kOutput, calls=%fused_computation.39 | convolution fusion | flops 1352924672 | bytes 8394752 | tf_op jit(solution)/shard_map/dot_general | solution.py:17
  80.4 26.6 %all-gather.13.cloned.1.call-done = bf16[5120,256]{1,0:T(8,128)(2,1)} async-done(((bf16[640,256]{1,0:T(8,128)(2,1)}), bf16[5120,256]{1,0:T(8,128)(2,1)}) %all-gather.13.cloned.1.call-update) | async-done | bytes 2621456 | tf_op jit(solution)/shard_map/all_gather | solution.py:54
  107.0 42.8 %all-gather.7.cloned.1.call-done = bf16[512,5120]{1,0:T(8,128)(2,1)} async-done(((bf16[64,5120]{1,0:T(8,128)(2,1)}), bf16[512,5120]{1,0:T(8,128)(2,1)}) %all-gather.7.cloned.1.call-update) | async-done | bytes 5242896 | tf_op jit(solution)/shard_map/all_gather | solution.py:49
  149.7 5.7 %multiply_reduce_fusion = (f32[512]{0:T(512)S(1)}, f32[512,256]{0,1:T(8,128)}) fusion(bf16[512,5120]{1,0:T(8,128)(2,1)} %all-gather.7.cloned.1.call-done, bf16[5120,256]{1,0:T(8,128)(2,1)} %all-gather.13.cloned.1.call-done), kind=kOutput, calls=%fused_computation.37 | convolution fusion | flops 1342438912 | bytes 8390656 | tf_op jit(solution)/shard_map/dot_general | solution.py:17
  155.4 11.8 %all-reduce.1 = (f32[512]{0:T(512)S(1)}, f32[512]{0:T(512)S(1)}) all-reduce(f32[512]{0:T(512)S(1)} %get-tuple-element.10, f32[512]{0:T(512)S(1)} %get-tuple-element.12), channel_id=1, replica_groups=mesh['seq'=8,'head'=4] {'head'}, use_global_device_ids=true, to_apply=%region_3.0 | all-reduce | flops 1024 | bytes 8192 | tf_op jit(solution)/shard_map/psum | solution.py:59
  167.3 0.1 multiply_convert_fusion.1
  167.4 1.1 multiply_convert_fusion
  168.5 0.9 fusion.36
  169.4 12.0 %all-gather.9.cloned.1.call-done = bf16[5120,256]{1,0:T(8,128)(2,1)} async-done(((bf16[640,256]{1,0:T(8,128)(2,1)}), bf16[5120,256]{1,0:T(8,128)(2,1)}) %all-gather.9.cloned.1.call-update) | async-done | bytes 2621456 | tf_op jit(solution)/shard_map/all_gather | solution.py:55
  181.5 5.6 %convolution_convert_fusion.1 = bf16[512,256]{0,1:T(8,128)(2,1)} fusion(bf16[512,5120]{1,0:T(8,128)(2,1)} %all-gather.7.cloned.1.call-done, bf16[5120,256]{1,0:T(8,128)(2,1)} %all-gather.9.cloned.1.call-done), kind=kOutput, calls=%fused_computation.26 | convolution fusion | flops 1342308352 | bytes 8126464 | tf_op jit(solution)/shard_map/dot_general | solution.py:17
  187.0 2.8 %convolution_convert_fusion = bf16[2,128,512]{2,1,0:T(8,128)(2,1)} fusion(bf16[512,2,128]{0,2,1:T(8,128)(2,1)} %bitcast.40, f32[2,512]{1,0:T(2,128)S(1)} %fusion.36, pred[512]{0:T(512)(128)(4,1)S(1)} %iota_compare_fusion, bf16[512,2,128]{0,2,1:T(8,128)(2,1)S(1)} %bitcast.37, bf16[512,2,128]{0,2,1:T(8,128)(2,1)S(1)} %bitcast.39), kind=kOutput, calls=%fused_computation.25 | convolution fusion | flops 271189504 | bytes 1053184 | tf_op jit(solution)/shard_map/hts,shd->thd/dot_general | solution.py:81
  190.6 1.3 fusion.16
  191.9 1.3 fusion.15
  193.3 2.6 %copy.24 = bf16[4,256,1280]{2,1,0:T(8,128)(2,1)} copy(bf16[4,256,1280]{1,2,0:T(8,128)(2,1)S(1)} %bitcast.32) | data formatting | bytes 5242880 | tf_op jit(solution)/shard_map/all_to_all | solution.py:86
  195.9 22.2 %all-gather.15.cloned.1.call-done = bf16[512,1024]{0,1:T(8,128)(2,1)} async-done(((bf16[512,256]{0,1:T(8,128)(2,1)}), bf16[512,1024]{0,1:T(8,128)(2,1)}) %all-gather.15.cloned.1.call-update) | async-done | bytes 1048592 | tf_op jit(solution)/shard_map/all_gather | solution.py:88
  218.0 4.3 %convert_reduce_fusion.1 = (f32[512]{0:T(512)S(1)}, f32[512]{0:T(512)S(1)}, bf16[512,1280]{1,0:T(8,128)(2,1)S(1)}) fusion(bf16[512,1024]{0,1:T(8,128)(2,1)} %all-gather.15.cloned.1.call-done, bf16[1024,1280]{1,0:T(8,128)(2,1)} %bitcast.34, bf16[512,5120]{1,0:T(8,128)(2,1)} %param.12, s32[]{:T(128)S(6)} %select_n.7), kind=kOutput, calls=%fused_computation.10 | convolution fusion | flops 1346763776 | bytes 6295556 | tf_op jit(solution)/shard_map/dot_general | solution.py:87
  222.3 10.2 %all-reduce = (f32[512]{0:T(512)S(1)}, f32[512]{0:T(512)S(1)}) all-reduce(f32[512]{0:T(512)S(1)} %get-tuple-element.3, f32[512]{0:T(512)S(1)} %get-tuple-element.2), channel_id=1, replica_groups=mesh['seq'=8,'head'=4] {'head'}, use_global_device_ids=true, to_apply=%region_11.12 | all-reduce | flops 1024 | bytes 8192 | tf_op jit(solution)/shard_map/psum | solution.py:104
  232.5 1.6 fusion.11
  (23 shorter events, 0.3 us)
Async XLA Ops:
  7.2 36.0 %all-gather.17.cloned.1.call-start = ((), (), s32[]{:S(2)}) async-start(), calls=%async_computation.6 | async-start | bytes 2949120 | tf_op jit(solution)/shard_map/all_gather | solution.py:85
  9.1 66.0 %all-gather.11.cloned.1.call-start = ((), (), s32[]{:S(2)}) async-start(), calls=%async_computation.3 | async-start | bytes 2949120 | tf_op jit(solution)/shard_map/all_gather | solution.py:48
  9.9 97.1 %all-gather.13.cloned.1.call-start = ((), (), s32[]{:S(2)}) async-start(), calls=%async_computation.4 | async-start | bytes 2949120 | tf_op jit(solution)/shard_map/all_gather | solution.py:54
  10.6 139.1 %all-gather.7.cloned.1.call-start = ((), (), s32[]{:S(2)}) async-start(), calls=%async_computation.1 | async-start | bytes 5898240 | tf_op jit(solution)/shard_map/all_gather | solution.py:49
  11.2 170.3 %all-gather.9.cloned.1.call-start = ((), (), s32[]{:S(2)}) async-start(), calls=%async_computation.2 | async-start | bytes 2949120 | tf_op jit(solution)/shard_map/all_gather | solution.py:55
  12.4 4.0 %copy-start = (bf16[512,5120]{1,0:T(8,128)(2,1)S(1)}, bf16[512,5120]{1,0:T(8,128)(2,1)}, u32[]{:S(2)}) copy-start(bf16[512,5120]{1,0:T(8,128)(2,1)} %param.12) | copy-start | bytes 15728644
  43.2 150.1 %all-to-all-start = ((bf16[256,4,1280]{0,2,1:T(8,128)(2,1)}), bf16[256,4,1280]{0,2,1:T(8,128)(2,1)S(1)}, u32[]{:S(2)}, u32[]{:S(2)}) async-start(bf16[256,4,1280]{0,2,1:T(8,128)(2,1)} %bitcast.33), calls=%async_computation | async-start | bytes 5242880 | tf_op jit(solution)/shard_map/all_to_all | solution.py:86
  47.8 170.2 %all-gather.15.cloned.1.call-start = ((), (), s32[]{:S(2)}) async-start(), calls=%async_computation.5 | async-start | bytes 1310720 | tf_op jit(solution)/shard_map/all_gather | solution.py:88
  80.4 86.9 %copy-start.3 = (f32[256]{0:T(256)S(1)}, f32[256]{0:T(256)}, u32[]{:S(2)}) copy-start(f32[256]{0:T(256)} %param.20) | copy-start | bytes 3076
  80.4 87.0 %copy-start.4 = (f32[256]{0:T(256)S(1)}, f32[256]{0:T(256)}, u32[]{:S(2)}) copy-start(f32[256]{0:T(256)} %param.21) | copy-start | bytes 3076
  187.0 3.6 %copy-start.2 = (f32[2,1280]{1,0:T(2,128)S(1)}, f32[2,1280]{1,0:T(2,128)}, u32[]{:S(2)}) copy-start(f32[2,1280]{1,0:T(2,128)} %param.23) | copy-start | bytes 30724
  222.3 11.8 %copy-start.1 = (bf16[512,1280]{1,0:T(8,128)(2,1)}, bf16[512,1280]{1,0:T(8,128)(2,1)S(1)}, u32[]{:S(2)}) copy-start(bf16[512,1280]{1,0:T(8,128)(2,1)S(1)} %get-tuple-element.14) | copy-start | bytes 3932164
Sparse Core Ops, SparseCore 0:
  10.4 32.6 all-gather.16
  45.0 29.9 all-gather.10
  77.0 29.9 all-gather.12
  108.7 40.9 all-gather.6
  151.5 29.9 all-gather.8
  190.0 27.9 all-gather.14
where the time goes:
time: 241 us
  waiting for transfers between devices  158 us (66%)
  matrix products  27.1 us (11%)
  blocking collectives  22 us (9%)
  between operations  15.5 us (6%)
  other arithmetic  7.88 us (3%)
  local copies, waits for them, and re-layouts  5.11 us (2%)
  starting transfers between devices  4.79 us (2%)
    all_gather x1, waiting for transfers between devices, on_device(): whole_text = lax.all_gather(context, 'seq', axis=0, tiled=True)  42.8 us
    all_gather x1, waiting for transfers between devices, on_device(): lax.all_gather(query_weight, 'seq', axis=0, tiled=True)  27.3 us
    all_gather x1, waiting for transfers between devices, on_device(): lax.all_gather(key_weight, 'seq', axis=0, tiled=True)  26.6 us
    all_gather x1, waiting for transfers between devices, on_device(): wide_rows = lax.all_gather(out_weight, 'seq', axis=1, tiled=True)  25.2 us
    all_gather x1, waiting for transfers between devices, on_device(): lax.all_gather(attended, 'head', axis=1, tiled=True)  22.2 us
    dot_general x3, matrix products, add_rows(): return jnp.dot(left, piece, preferred_element_type=jnp.float32)  16.5 us
    all_gather x1, waiting for transfers between devices, on_device(): lax.all_gather(value_weight, 'seq', axis=0, tiled=True)  12 us
    psum x1, blocking collectives, on_device(): lax.psum((jnp.sum(queries * queries, axis=1), jnp.sum(key_proj * key_proj...  11.8 us
  transfers between devices with their start and end apart: 7, of which 6 were waited for; matrix products, arithmetic and copies ran while one was open for 13% of the time, Pallas kernels for 0%

commit v1 on v0

v1 whole, which is shorter than its diff:
```python
import functools

import jax
import jax.numpy as jnp
from jax import lax
from jax.experimental import pallas as pl
from jax.experimental.pallas import tpu as pltpu
from jax.sharding import PartitionSpec as P

HD = 128
FREQ = 256
LANES = 128
F32 = jnp.float32
BF16 = jnp.bfloat16
MESH_ID = pl.DeviceIdType.MESH


def flip(index, mask):
    bit = 1
    while bit <= mask:
        if mask & bit:
            index = index + bit - 2 * bit * ((index // bit) % 2)
        bit *= 2
    return index


def rows_to_lanes(column, tall):
    return jnp.transpose(jnp.broadcast_to(column, (tall, LANES)))[:8]


def body(
    n_seq, n_head, chunks,
    valid, video, ctx, qw, kw, vw, ow, qg, kg, act, tw, mod, vpart,
    resid_out, mod_out,
    vid, normed, ctxg, qwg, part, pair, rsg, own_kv, kvg, spread, owg, attg,
    queries, qsq, ksq, stat, shsc,
    vid_sem, loc_sem, ctx_s, ctx_r, qw_s, qw_r, pr_s, pr_r, rs_s, rs_r, kv_s, kv_r,
    sp_s, sp_r, oz_s, oz_r, og_s, og_r, ksq_s, ksq_r, qsq_s, qsq_r, at_s, at_r, st_s, st_r,
):
    s = lax.axis_index("seq")
    z = lax.axis_index("head")
    core = s % 2
    chip = s // 2
    n_chip = n_seq // 2
    ratio = n_seq // n_head
    tok, width = vid.shape
    depth = qw.shape[0]
    att = qw.shape[1]
    text = ctx.shape[-2]
    sent = []

    def to_seq(k):
        return (flip(s, k), z)

    def to_head(k):
        return (s, flip(z, k))

    def remote(src, dst, ssem, rsem, dev):
        return pltpu.make_async_remote_copy(
            src_ref=src, dst_ref=dst, send_sem=ssem, recv_sem=rsem,
            device_id=dev, device_id_type=MESH_ID,
        )

    def push(src, dst, ssem, rsem, dev):
        copy = remote(src, dst, ssem, rsem, dev)
        copy.start()
        sent.append(copy)

    def arrived(dst, ssem, rsem, dev):
        remote(dst, dst, ssem, rsem, dev).wait_recv()

    def gather_start(slot, ssem, rsem):
        for k in range(2, n_seq, 2):
            push(slot(s), slot(s), ssem.at[k], rsem.at[k], to_seq(k))
        push(slot(s), slot(s), ssem.at[1], rsem.at[1], to_seq(1))

    def gather_relay(slot, ssem, rsem):
        for k in range(2, n_seq, 2):
            arrived(slot(flip(s, k)), ssem.at[k], rsem.at[k], to_seq(k))
            push(slot(flip(s, k)), slot(flip(s, k)), ssem.at[k + 1], rsem.at[k + 1], to_seq(1))

    def gather_end(slot, ssem, rsem):
        for k in range(1, n_seq, 2):
            arrived(slot(flip(s, k)), ssem.at[k], rsem.at[k], to_seq(1))

    load = pltpu.make_async_copy(video, vid, vid_sem)
    load.start()

    def qw_slot(p):
        return qwg.at[pl.ds(pl.multiple_of(p * depth, depth), depth), :]

    own_qw = pltpu.make_async_copy(qw, qw_slot(s), loc_sem.at[0])
    own_qw.start()
    own_ctx = pltpu.make_async_copy(ctx.at[s], ctxg.at[s], loc_sem.at[1])
    own_ctx.start()
    piece = ow.shape[0] // n_seq

    def ow_piece(p):
        return pl.ds(pl.multiple_of(p * piece, piece), piece)

    own_spread = pltpu.make_async_copy(ow.at[ow_piece(s), :], spread.at[s], loc_sem.at[2])
    own_spread.start()

    barrier = pltpu.get_barrier_semaphore()
    for k in range(1, n_seq):
        pl.semaphore_signal(barrier, inc=1, device_id=to_seq(k), device_id_type=MESH_ID)
    for k in range(1, n_head):
        pl.semaphore_signal(barrier, inc=1, device_id=to_head(k), device_id_type=MESH_ID)
    pl.semaphore_wait(barrier, n_seq + n_head - 2)

    for k in range(1, n_seq):
        push(ctx.at[flip(s, k)], ctxg.at[s], ctx_s.at[k], ctx_r.at[k], to_seq(k))
    own_qw.wait()
    gather_start(qw_slot, qw_s, qw_r)
    for k in range(1, n_seq):
        push(ow.at[ow_piece(flip(s, k)), :], spread.at[s], sp_s.at[k], sp_r.at[k], to_seq(k))

    load.wait()
    strip = 16

    @pl.loop(0, tok // strip)
    def _(i):
        at = pl.ds(pl.multiple_of(i * strip, strip), strip)
        rows = vid[at, :].astype(F32)
        mean = jnp.mean(rows, axis=-1, keepdims=True)
        centred = rows - mean
        spread_ = jnp.mean(centred * centred, axis=-1, keepdims=True)
        normed[at, :] = (centred / jnp.sqrt(spread_ + 1e-06)).astype(BF16)

    own_ctx.wait()
    for k in range(1, n_seq):
        arrived(ctxg.at[flip(s, k)], ctx_s.at[k], ctx_r.at[k], to_seq(k))
    source = ctxg[...].reshape(n_seq * text, depth)
    keys = jnp.dot(source, kw[...], preferred_element_type=F32)
    part[:, :, :, :att] = keys.reshape(n_chip, 2, text, att)
    values = jnp.dot(source, vw[...], preferred_element_type=F32)
    part[:, :, :, att:] = values.reshape(n_chip, 2, text, att)
    push(part.at[:, 1 - core], pair, pr_s, pr_r, to_seq(1))

    for i in range(2):
        shsc[i] = mod[i : i + 1, :] + jnp.dot(act[...], tw[i], preferred_element_type=F32)[:8]

    arrived(pair, pr_s, pr_r, to_seq(1))
    for c in range(n_chip):
        rsg[0, c] = part[c, core] + pair[c]
    for k in range(1, n_chip):
        push(
            rsg.at[0, flip(chip, k)], rsg.at[k, chip], rs_s.at[k], rs_r.at[k], to_seq(2 * k)
        )

    own_spread.wait()
    for k in range(1, n_seq):
        arrived(spread.at[flip(s, k)], sp_s.at[k], sp_r.at[k], to_seq(k))

    def own_cols(zz):
        return pl.ds(zz * ratio, ratio)

    own_ow = pltpu.make_async_copy(
        spread.at[own_cols(z)], owg.at[:, z, ow_piece(s), :], loc_sem.at[3]
    )
    own_ow.start()
    for k in range(1, n_head):
        push(
            spread.at[own_cols(flip(z, k))], owg.at[:, z, ow_piece(s), :],
            oz_s.at[k], oz_r.at[k], to_head(k),
        )

    gather_relay(qw_slot, qw_s, qw_r)
    gather_end(qw_slot, qw_s, qw_r)
    queries[...] = jnp.dot(normed[...], qwg[...], preferred_element_type=F32)
    q_sum = jnp.sum(queries[...] * queries[...], axis=1, keepdims=True)
    qsq[0] = rows_to_lanes(q_sum, tok)

    total = rsg[0, chip]
    for k in range(1, n_chip):
        arrived(rsg.at[k, flip(chip, k)], rs_s.at[k], rs_r.at[k], to_seq(2 * k))
        total = total + rsg[k, flip(chip, k)]
    key_rows = total[:, :att]
    k_sum = jnp.sum(key_rows * key_rows, axis=1, keepdims=True)
    ksq[0] = jnp.broadcast_to(k_sum, (text, LANES))
    for k in range(1, n_head):
        push(ksq.at[0], ksq.at[k], ksq_s.at[k], ksq_r.at[k], to_head(k))
    for k in range(1, n_head):
        push(qsq.at[0], qsq.at[k], qsq_s.at[k], qsq_r.at[k], to_head(k))
    for k in range(1, n_head):
        arrived(ksq.at[k], ksq_s.at[k], ksq_r.at[k], to_head(k))
    k_mean = jnp.sum(ksq[...], axis=0)[:, :1] / (att * n_head)
    own_kv[:, :att] = (key_rows / jnp.sqrt(k_mean + 1e-06) * kg[...]).astype(BF16)
    own_kv[:, att:] = total[:, att:].astype(BF16)
    kvg[s] = own_kv[...]

    def kv_slot(p):
        return kvg.at[p]

    gather_start(kv_slot, kv_s, kv_r)

    for k in range(1, n_head):
        arrived(qsq.at[k], qsq_s.at[k], qsq_r.at[k], to_head(k))
    q_lane = jnp.sum(qsq[...], axis=0)
    q_mean = jnp.transpose(q_lane)[:, :1] / (att * n_head)
    q_normed = (queries[...] / jnp.sqrt(q_mean + 1e-06) * qg[...]).astype(BF16)

    own_ow.wait()
    for k in range(1, n_head):
        arrived(owg.at[:, flip(z, k), ow_piece(s), :], oz_s.at[k], oz_r.at[k], to_head(k))

    def ow_slot(p):
        return owg.at[:, :, ow_piece(p), :]

    gather_relay(kv_slot, kv_s, kv_r)
    gather_start(ow_slot, og_s, og_r)
    gather_end(kv_slot, kv_s, kv_r)

    every = kvg[...].reshape(n_seq * text, 2 * att)
    all_text = n_seq * text
    seen = lax.broadcasted_iota(jnp.int32, (1, all_text), 1) < valid[0]
    step = tok // chunks
    for c in range(chunks):
        at = slice(c * step, (c + 1) * step)
        for h in range(att // HD):
            lanes = slice(h * HD, (h + 1) * HD)
            scores = lax.dot_general(
                q_normed[at, lanes], every[:, lanes], (((1,), (1,)), ((), ())),
                preferred_element_type=F32,
            ) * HD ** (-0.5)
            scores = jnp.where(seen, scores, F32(-1e30))
            shifted = jnp.exp(scores - jnp.max(scores, axis=-1, keepdims=True))
            weights = (shifted / jnp.sum(shifted, axis=-1, keepdims=True)).astype(BF16)
            attg[0, at, lanes] = jnp.dot(
                weights, every[:, att + h * HD : att + (h + 1) * HD],
                preferred_element_type=F32,
            ).astype(BF16)
        for k in range(1, n_head):
            push(
                attg.at[0, at], attg.at[k, at],
                at_s.at[c, k], at_r.at[c, k], to_head(k),
            )
    gather_relay(ow_slot, og_s, og_r)
    gather_end(ow_slot, og_s, og_r)

    cols = owg.shape[3]
    sums = []
    squares = []
    for c in range(chunks):
        at = slice(c * step, (c + 1) * step)
        for k in range(1, n_head):
            arrived(attg.at[k, at], at_s.at[c, k], at_r.at[c, k], to_head(k))
        row_sum = jnp.zeros((step, 1), F32)
        row_sq = jnp.zeros((step, 1), F32)
        for j in range(ratio):
            here = slice(j * cols, (j + 1) * cols)
            projected = jnp.dot(attg[0, at], owg[j, z], preferred_element_type=F32)
            for k in range(1, n_head):
                projected = projected + jnp.dot(
                    attg[k, at], owg[j, flip(z, k)], preferred_element_type=F32
                )
            rounded = (vpart[at, here].astype(F32) + projected).astype(BF16)
            resid_out[at, here] = rounded
            wide = rounded.astype(F32)
            row_sum = row_sum + jnp.sum(wide, axis=1, keepdims=True)
            row_sq = row_sq + jnp.sum(wide * wide, axis=1, keepdims=True)
        sums.append(row_sum)
        squares.append(row_sq)
    stat[0, :8] = rows_to_lanes(jnp.concatenate(sums, axis=0), tok)
    stat[0, 8:] = rows_to_lanes(jnp.concatenate(squares, axis=0), tok)
    for k in range(1, n_head):
        push(stat.at[0], stat.at[k], st_s.at[k], st_r.at[k], to_head(k))
    for k in range(1, n_head):
        arrived(stat.at[k], st_s.at[k], st_r.at[k], to_head(k))
    both = jnp.sum(stat[...], axis=0) / (mod_out.shape[1] * n_head)
    mean2 = both[:8]
    inverse = 1.0 / jnp.sqrt(both[8:] - mean2 * mean2 + 1e-06)
    mean_col = jnp.transpose(mean2)[:, :1]
    inv_col = jnp.transpose(inverse)[:, :1]
    for c in range(chunks):
        at = slice(c * step, (c + 1) * step)
        wide = resid_out[at, :].astype(F32)
        mod_out[at, :] = (
            (wide - mean_col[at]) * inv_col[at] * (1.0 + shsc[1, :1, :]) + shsc[0, :1, :]
        ).astype(BF16)
    for copy in sent:
        copy.wait_send()


def on_device(
    n_seq,
    n_head,
    video_rows,
    context,
    valid_length,
    timestep,
    query_weight,
    key_weight,
    value_weight,
    out_weight,
    query_gain,
    key_gain,
    time_weight,
    modulation,
):
    tok, width = video_rows.shape
    text = context.shape[0]
    depth, att = query_weight.shape
    cols = out_weight.shape[1]
    part_width = modulation.shape[1]
    ratio = n_seq // n_head
    n_chip = n_seq // 2
    chunks = 4
    piece = out_weight.shape[0] // n_seq
    half = FREQ // 2
    freqs = jnp.exp(-jnp.log(10000.0) * jnp.arange(half, dtype=F32) / half)
    angles = timestep[0].astype(F32) * freqs
    embedding = jnp.concatenate([jnp.cos(angles), jnp.sin(angles)])
    act = jnp.broadcast_to(jax.nn.silu(embedding).astype(BF16)[None, :], (16, FREQ))
    blocks = context.reshape(text, n_seq, depth).transpose(1, 0, 2)
    vpart = lax.dynamic_slice_in_dim(
        video_rows, lax.axis_index("head") * part_width, part_width, 1
    )
    vmem = pl.BlockSpec(memory_space=pltpu.VMEM)
    dma = pltpu.SemaphoreType.DMA
    seq_sems = [dma((n_seq,))] * 2
    head_sems = [dma((n_head,))] * 2
    return pl.pallas_call(
        functools.partial(body, n_seq, n_head, chunks),
        out_shape=[jax.ShapeDtypeStruct((tok, part_width), BF16)] * 2,
        in_specs=[
            pl.BlockSpec(memory_space=pltpu.SMEM),
            pl.BlockSpec(memory_space=pl.ANY),
        ]
        + [vmem] * 11,
        out_specs=[vmem] * 2,
        scratch_shapes=[
            pltpu.VMEM((tok, width), BF16),
            pltpu.VMEM((tok, width), BF16),
            pltpu.VMEM((n_seq, text, depth), BF16),
            pltpu.VMEM((n_seq * depth, att), BF16),
            pltpu.VMEM((n_chip, 2, text, 2 * att), F32),
            pltpu.VMEM((n_chip, text, 2 * att), F32),
            pltpu.VMEM((n_chip, n_chip, text, 2 * att), F32),
            pltpu.VMEM((text, 2 * att), BF16),
            pltpu.VMEM((n_seq, text, 2 * att), BF16),
            pltpu.VMEM((n_seq, piece, cols), BF16),
            pltpu.VMEM((ratio, n_head, out_weight.shape[0], cols), BF16),
            pltpu.VMEM((n_head, tok, att), BF16),
            pltpu.VMEM((tok, att), F32),
            pltpu.VMEM((n_head, 8, tok), F32),
            pltpu.VMEM((n_head, text, LANES), F32),
            pltpu.VMEM((n_head, 16, tok), F32),
            pltpu.VMEM((2, 8, part_width), F32),
            dma,
            dma((4,)),
            *seq_sems,
            *seq_sems,
            dma,
            dma,
            *[dma((n_chip,))] * 2,
            *seq_sems,
            *seq_sems,
            *head_sems,
            *seq_sems,
            *head_sems,
            *head_sems,
            *[dma((chunks, n_head))] * 2,
            *head_sems,
        ],
        compiler_params=pltpu.CompilerParams(
            collective_id=0, has_side_effects=True, vmem_limit_bytes=60 * 1024 * 1024
        ),
    )(
        valid_length,
        video_rows,
        blocks,
        query_weight,
        key_weight,
        value_weight,
        out_weight,
        query_gain[None, :],
        key_gain[None, :],
        act,
        time_weight,
        modulation,
        vpart,
    )


def solution(mesh):
    in_specs = (
        P("seq", None),
        P("seq", None),
        P(),
        P(),
        P("seq", "head"),
        P("seq", "head"),
        P("seq", "head"),
        P("head", "seq"),
        P("head"),
        P("head"),
        P(None, None, "head"),
        P(None, "head"),
    )
    out_specs = (P("seq", "head"), P("seq", "head"))
    return jax.shard_map(
        functools.partial(on_device, mesh.shape["seq"], mesh.shape["head"]),
        mesh=mesh, in_specs=in_specs, out_specs=out_specs, check_vma=False,
    )
```

time: 241 us -> 99.8 us (0.41)
  waiting for transfers between devices: 158 us -> 0 us
  Pallas kernels: 0 us -> 88.9 us
  matrix products: 27.1 us -> 0 us
  blocking collectives: 22 us -> 0 us
  between operations: 15.5 us -> 1.95 us
  other arithmetic: 7.88 us -> 0.06 us
  starting transfers between devices: 4.79 us -> 0 us
  local copies, waits for them, and re-layouts: 5.11 us -> 8.68 us
    all_gather x6 -> x0, waiting for transfers between devices: 156 us -> none  [the longest x1 42.8 us: on_device(): whole_text = lax.all_gather(context, 'seq', axis=0, tiled=True)]
    pallas_call x0 -> x1, Pallas kernels: none -> 88.9 us  [on_device(): pl.pallas_call(functools.partial(body, n_seq, n_head, chunks), out_shape=...]
    dot_general x7 -> x0, matrix products: 26.2 us -> none  [the longest x3 16.5 us: add_rows(): return jnp.dot(left, piece, preferred_element_type=jnp.float32)]
    psum x2 -> x0, blocking collectives: 22 us -> none  [the longest x1 11.8 us: on_device(): lax.psum((jnp.sum(queries * queries, axis=1), jnp.sum(key_proj * key_proj...]
    reduce_sum x2 -> x0, other arithmetic: 4.91 us -> none  [the longest x1 3.4 us: layer_norm(): mean = jnp.mean(rows, axis=-1, keepdims=True)]
    all_to_all x1 -> x0, starting transfers between devices: 4.6 us -> none  [on_device(): lax.all_to_all(wide_rows, 'head', split_axis=1, concat_axis=0, tiled=True)]
    convert_element_type x4 -> x1, other arithmetic: 2.87 us -> 0.01 us  [on_device(): jax.nn.silu(embedding).astype(BF16)[None, :]]
    all_to_all x1 -> x0, local copies, waits for them, and re-layouts: 2.59 us -> none  [on_device(): lax.all_to_all(wide_rows, 'head', split_axis=1, concat_axis=0, tiled=True)]
  transfers between devices with their start and end apart: 7 -> 0, of which waited for: 6 -> 0; matrix products, arithmetic and copies ran while one was open for 13% -> 0% of each run, Pallas kernels for 0% -> 0%
where the time goes in v1:
time: 99.8 us; the launch traced here: 99.6 us
  Pallas kernels  88.9 us (89%)
  local copies, waits for them, and re-layouts  8.68 us (9%)
  between operations  1.95 us (2%)
    pallas_call x1, Pallas kernels, on_device(): pl.pallas_call(functools.partial(body, n_seq, n_head, chunks), out_shape=...  88.9 us
    unnamed x4, local copies, waits for them, and re-layouts  3.62 us
    dynamic_slice x1, local copies, waits for them, and re-layouts, on_device(): lax.dynamic_slice_in_dim(video_rows, lax.axis_index('head') * part_width,...  2.46 us

profile of v1, /device:TPU:0, one launch (start us, length us, event | category | flops | bytes accessed | tf_op | source)
XLA Modules:
  0.0 99.6 jit_solution(9326970543521067622)
XLA Ops:
  2.0 0.6 broadcast_in_dim.14.act
  2.6 2.0 %copy.17 = bf16[8,8,8,640]{3,2,0,1:T(8,128)(2,1)} copy(bf16[8,8,8,640]{3,2,1,0:T(8,128)(2,1)} %bitcast.11) | data formatting | bytes 1310720 | tf_op jit(solution)/shard_map/reshape | solution.py:315
  4.6 2.5 %constant_dynamic-slice_fusion.vpart = bf16[512,1280]{1,0:T(8,128)(2,1)} fusion(bf16[512,5120]{1,0:T(8,128)(2,1)} %video.1, s32[]{:T(128)S(6)} %select_n.3), kind=kLoop, calls=%fused_computation.5 | loop fusion | bytes 2621444 | tf_op jit(solution)/shard_map/dynamic_slice | solution.py:316
  7.1 88.9 %shard_map.131 = (bf16[512,1280]{1,0:T(8,128)(2,1)}, bf16[512,1280]{1,0:T(8,128)(2,1)}) custom-call(s32[1]{0:T(128)S(6)} %copy.20.valid, bf16[512,5120]{1,0:T(8,128)(2,1)} %video.1, bf16[8,64,640]{2,1,0:T(8,128)(2,1)} %bitcast.10, bf16[640,256]{1,0:T(8,128)(2,1)} %qw.1, bf16[640,256]{1,0:T(8,128)(2,1)} %kw.1, bf16[640,256]{1,0:T(8,128)(2,1)} %vw.1, ...), custom_call_target="tpu_custom_call" | custom-call | tf_op jit(solution)/shard_map/pallas_call | solution.py:323
  95.9 0.0 copy-start
  95.9 2.6 %copy.22 = bf16[512,1280]{1,0:T(8,128)(2,1)} copy(bf16[512,1280]{1,0:T(8,128)(2,1)} %get-tuple-element.6) | data formatting | bytes 2621440
  98.5 0.0 copy-done
  98.5 1.1 %copy.23 = bf16[512,1280]{1,0:T(8,128)(2,1)} copy(bf16[512,1280]{1,0:T(8,128)(2,1)S(1)} %copy-done) | data formatting | bytes 2621440
  (2 shorter events, 0.1 us)
Async XLA Ops:
  95.9 2.6 %copy-start = (bf16[512,1280]{1,0:T(8,128)(2,1)S(1)}, bf16[512,1280]{1,0:T(8,128)(2,1)}, u32[]{:S(2)}) copy-start(bf16[512,1280]{1,0:T(8,128)(2,1)} %get-tuple-element.7) | copy-start | bytes 3932164
